TPU v7x, 512 devices: a whole 4x4x16 slice. The times are simulated.
512 devices in a mesh: tm: 128 (over x, z, core), space: 4 (over y).
Axes of the slice: x: 4, y: 4, z: 16, core: 2. Of those that a mesh axis runs over, the one named last changes fastest.
Arguments:
- forcing: bfloat16 [2048, 256, 256], P('tm', 'space'), may hold values from -0.59765625 to 0.59765625
- starting_heat: bfloat16 [256, 256], P('space'), may hold values from -3 to 3, as said below
Outputs:
- heat_history: float32 [2048, 256, 256], P('tm', 'space')
- history: float32 [2, 512], P(None, 'tm')
- change: float32 [2, 512], P(None, 'tm')
Inputs may be any that keep to these rules, and one draw needn't show every extreme that they name: starting_heat is a combination of the 64 sine modes with both indices from 1 to 8, scaled so that its largest magnitude is 3.
All inputs are finite; a program needn't handle non-finite values.
Results may differ from a plain program's by a relative error of at most 0.0016.
Values may be sent and summed in bfloat16 or wider, within the bound.
A program may use at most 64 MiB of HBM per device.

v0:
```python
import math

import jax
import jax.numpy as jnp
from jax import lax
from jax.sharding import Mesh
from jax.sharding import PartitionSpec as P

FINE_FACTOR = 4
COARSE_FACTOR = 4
ITERS = 2
TM = ("tm_0", "tm_1", "tm_2")


DURATION = 0.004


def passed_along(block, axis, distance):
    devices = range(lax.axis_size(axis))
    route = [(i - distance, i) for i in devices if i - distance in devices]
    return lax.ppermute(block, axis, route)


def nothing_yet(array, identity):
    return jax.tree.map(
        lambda a, e: jnp.broadcast_to(jnp.asarray(e, a.dtype), a.shape), array, identity
    )


def carried_in(array, axes, combine, identity, reverse):
    before = start = nothing_yet(array, identity)
    running = array
    for axis in reversed(axes):
        devices, mine = lax.axis_size(axis), lax.axis_index(axis)
        pieces = jax.tree.map(lambda part: lax.all_gather(part, axis), running)
        inside, running = start, start
        for k in reversed(range(devices)) if reverse else range(devices):
            passed = k > mine if reverse else k < mine
            running = combine(running, jax.tree.map(lambda part: part[k], pieces))
            inside = jax.tree.map(lambda new, old: jnp.where(passed, new, old), running, inside)
        before = combine(inside, before)
    return before


def sine_table(sample_locations, number_type):
    numbers = jnp.arange(1, sample_locations + 1, dtype=jnp.int32)
    product = numbers[:, None] * numbers[None, :] % (2 * (sample_locations + 1))
    angles = jnp.pi * product.astype(jnp.float32) / (sample_locations + 1)
    return (math.sqrt(2.0 / (sample_locations + 1)) * jnp.sin(angles)).astype(number_type)


def eigenvalues(sample_locations, first_mode, mode_count):
    numbers = (first_mode + jnp.arange(mode_count, dtype=jnp.int32) + 1).astype(jnp.float32)
    halves = jnp.sin(jnp.pi * numbers / (2 * (sample_locations + 1)))
    return 4.0 * (sample_locations + 1) ** 2 * halves * halves


def smoothing_pass(starts, sources, factor):
    current = starts
    visited = []
    for column in range(sources.shape[1] - 1):
        current = factor * current + sources[:, column]
        visited.append(current)
    return visited


def compose_powers(earlier, later):
    return (earlier[0] * later[0], later[0] * earlier[1] + later[1])


def per_device(forcing, starting_heat):
    step_count, row_count, sample_locations = forcing.shape
    block_width = sample_locations // lax.axis_size("space")
    intervals = step_count // FINE_FACTOR
    blocks = intervals // COARSE_FACTOR
    steps_all = step_count * lax.axis_size(TM)
    table_half = sine_table(sample_locations, jnp.bfloat16)
    table_full = sine_table(sample_locations, jnp.float32)
    stacked = jnp.concatenate([starting_heat[None], forcing], axis=0)
    halved = jnp.dot(
        stacked.reshape(-1, sample_locations), table_half, preferred_element_type=jnp.float32
    )
    halved = halved.astype(jnp.bfloat16).reshape(step_count + 1, row_count, sample_locations)
    turned = lax.all_to_all(halved, "space", split_axis=2, concat_axis=1, tiled=True)
    spectra = jnp.einsum("xi,tiy->txy", table_half, turned, preferred_element_type=jnp.float32)
    first_mode = lax.axis_index("space") * block_width
    decay_rates = (
        eigenvalues(sample_locations, 0, sample_locations)[:, None]
        + eigenvalues(sample_locations, first_mode, block_width)[None, :]
    )
    increment_duration = DURATION / steps_all
    per_increment_factor = 1.0 / (1.0 + increment_duration * decay_rates)
    mid_gain = 1.0 / (1.0 + FINE_FACTOR * increment_duration * decay_rates)
    top_gain = 1.0 / (1.0 + FINE_FACTOR * COARSE_FACTOR * increment_duration * decay_rates)
    block_gain = top_gain
    for block_index in range(1, blocks):
        block_gain = block_gain * top_gain
    start_field = spectra[0]
    sources = (per_increment_factor * spectra[1:]).reshape(
        intervals, FINE_FACTOR, sample_locations, block_width
    )
    at_start = lax.axis_index(TM) == 0
    values = jnp.zeros((intervals, sample_locations, block_width), jnp.float32)
    pinned_boundary = jnp.where(at_start, start_field, jnp.zeros_like(start_field))
    norm_rows = []
    corr_rows = []
    value_rows = []
    for iteration in range(ITERS):
        ends_rest = smoothing_pass(values[:-1], sources[1:], per_increment_factor)[-1]
        relaxed_rest = per_increment_factor * ends_rest + sources[1:, -1]
        arrived = passed_along(relaxed_rest[-1], TM, 1)
        ends_first = smoothing_pass(pinned_boundary[None], sources[:1], per_increment_factor)[-1]
        relaxed = jnp.concatenate(
            [per_increment_factor * ends_first + sources[:1, -1], relaxed_rest], 0
        )
        arrived = jnp.where(at_start, start_field, arrived)
        ends_two = smoothing_pass(
            jnp.concatenate([arrived[None], relaxed[:-1]], 0), sources, per_increment_factor
        )[-1]
        residual = sources[:, -1] + per_increment_factor * ends_two - relaxed
        local_norms = jnp.sum(residual * residual, axis=(1, 2))
        coarse_rhs = residual.reshape(blocks, COARSE_FACTOR, sample_locations, block_width)
        running = coarse_rhs[:, 0]
        for column in range(1, COARSE_FACTOR):
            running = mid_gain * running + coarse_rhs[:, column]
        local_end = running[0]
        for block_index in range(1, blocks):
            local_end = top_gain * local_end + running[block_index]
        prefix = carried_in(
            (block_gain, local_end),
            TM,
            compose_powers,
            (jnp.ones_like(block_gain), jnp.zeros_like(local_end)),
            False,
        )
        incoming_value = prefix[1]
        coarse_list = []
        current = incoming_value
        for block_index in range(blocks):
            current = top_gain * current + running[block_index]
            coarse_list.append(current)
        coarse_values = jnp.stack(coarse_list)
        begins = jnp.concatenate([incoming_value[None], coarse_values[:-1]], 0)
        pieces = smoothing_pass(begins, coarse_rhs, mid_gain)
        correction = jnp.stack(pieces + [coarse_values], axis=1).reshape(
            intervals, sample_locations, block_width
        )
        values = relaxed + correction
        corr_sq = jnp.sum(correction * correction, axis=(1, 2))
        value_sq = jnp.sum(values * values, axis=(1, 2))
        norm_rows.append(local_norms)
        corr_rows.append(corr_sq)
        value_rows.append(value_sq)
        pinned_boundary = arrived + incoming_value
    starts = jnp.concatenate([pinned_boundary[None], values[:-1]], 0)
    inside = smoothing_pass(starts, sources, per_increment_factor)
    spectral_path = jnp.stack(inside + [values], axis=1).reshape(
        step_count, sample_locations, block_width
    )
    rows_back = jnp.einsum(
        "xi,tiy->txy", table_full, spectral_path, precision=lax.Precision.HIGHEST
    ).astype(jnp.bfloat16)
    returned = lax.all_to_all(rows_back, "space", split_axis=1, concat_axis=2, tiled=True)
    physical_rows = jnp.dot(
        returned.reshape(-1, sample_locations), table_half, preferred_element_type=jnp.float32
    )
    heat_history = physical_rows.reshape(step_count, row_count, sample_locations)
    norm_total, corr_total, value_total = lax.psum(
        (jnp.stack(norm_rows), jnp.stack(corr_rows), jnp.stack(value_rows)), "space"
    )
    history = jnp.sqrt(norm_total / (sample_locations * sample_locations))
    change = jnp.sqrt(corr_total / value_total)
    return (heat_history, history, change)


def solution(mesh):
    torus = Mesh(
        mesh.devices.reshape(4, 16, 2, mesh.shape["space"]), ("tm_0", "tm_1", "tm_2", "space")
    )
    in_specs = (P(TM, "space", None), P("space", None))
    out_specs = (P(TM, "space", None), P(None, TM), P(None, TM))
    return jax.shard_map(
        per_device, mesh=torus, in_specs=in_specs, out_specs=out_specs, check_vma=False
    )
```

profile of v0, /device:TPU:2, one launch (start us, length us, event | category | flops | bytes accessed | tf_op | source)
XLA Modules:
  0.0 344.0 jit_solution(6971806661333122464)
XLA Ops:
  10.6 1.6 reshape.2401
  12.2 4.5 %all-to-all-start = ((bf16[4,2,34816]{2,1,0:T(2,128)(2,1)}), bf16[4,2,34816]{2,1,0:T(2,128)(2,1)S(1)}, u32[]{:S(2)}, u32[]{:S(2)}) async-start(bf16[4,2,34816]{2,1,0:T(2,128)(2,1)} %reshape.2401), calls=%async_computation | async-start | bytes 1114112 | tf_op jit(solution)/shard_map/all_to_all | solution.py:84
  16.9 9.7 %all-to-all-done = bf16[4,2,34816]{2,1,0:T(2,128)(2,1)S(1)} async-done(((bf16[4,2,34816]{2,1,0:T(2,128)(2,1)}), bf16[4,2,34816]{2,1,0:T(2,128)(2,1)S(1)}, u32[]{:S(2)}, u32[]{:S(2)}) %all-to-all-start) | async-done | bytes 557088 | tf_op jit(solution)/shard_map/all_to_all | solution.py:84
  27.8 1.9 copy.55
  29.7 2.1 all_to_all.27
  33.5 1.9 collective-permute-start
  35.6 9.5 %collective-permute-done = f32[256,64]{0,1:T(8,128)S(1)} collective-permute-done((f32[256,64]{0,1:T(8,128)S(1)}, f32[256,64]{0,1:T(8,128)S(1)}, u32[]{:S(2)}, u32[]{:S(2)}) %collective-permute-start) | collective-permute-done | bytes 65568 | tf_op jit(solution)/shard_map/ppermute | solution.py:21
  45.7 1.9 all_gather.18
  47.6 1.9 all_gather.21
  51.1 67.7 %all-gather.4.cloned.1.call-done = f32[16,256,64]{1,2,0:T(8,128)} async-done(((f32[1,256,64]{1,2,0:T(8,128)}), f32[16,256,64]{1,2,0:T(8,128)}) %all-gather.4.cloned.1.call-update) | async-done | bytes 1048592 | tf_op jit(solution)/shard_map/all_gather | solution.py:35
  118.7 69.9 %all-gather.6.cloned.1.call-done = f32[16,256,64]{1,2,0:T(8,128)} async-done(((f32[1,256,64]{1,2,0:T(8,128)}), f32[16,256,64]{1,2,0:T(8,128)}) %all-gather.6.cloned.1.call-update) | async-done | bytes 1048592 | tf_op jit(solution)/shard_map/all_gather | solution.py:35
  188.6 1.7 multiply_add_fusion.17
  190.3 12.4 %all_gather.45 = f32[4,256,64]{1,2,0:T(8,128)S(1)} all-gather(f32[1,256,64]{1,2,0:T(8,128)S(1)} %get-tuple-element.32), channel_id=1, replica_groups=mesh['tm_0'=4,'tm_1'=16,'tm_2'=2,'space'=4] {'tm_0'}, dimensions={0}, use_global_device_ids=true | all-gather | bytes 327680 | tf_op jit(solution)/shard_map/all_gather | solution.py:35
  202.8 12.3 %all_gather.20 = f32[4,256,64]{1,2,0:T(8,128)S(1)} all-gather(f32[1,256,64]{1,2,0:T(8,128)S(1)} %slice_multiply_fusion.3), channel_id=1, replica_groups=mesh['tm_0'=4,'tm_1'=16,'tm_2'=2,'space'=4] {'tm_0'}, dimensions={0}, use_global_device_ids=true | all-gather | bytes 327680 | tf_op jit(solution)/shard_map/all_gather | solution.py:35
  218.6 1.9 collective-permute-start.1
  220.6 5.7 %collective-permute-done.1 = f32[256,64]{0,1:T(8,128)S(1)} collective-permute-done((f32[256,64]{0,1:T(8,128)S(1)}, f32[256,64]{0,1:T(8,128)S(1)}, u32[]{:S(2)}, u32[]{:S(2)}) %collective-permute-start.1) | collective-permute-done | bytes 65568 | tf_op jit(solution)/shard_map/ppermute | solution.py:21
  227.4 1.9 all_gather.46
  230.4 66.3 %all-gather.8.cloned.1.call-done = f32[16,256,64]{1,2,0:T(8,128)} async-done(((f32[1,256,64]{1,2,0:T(8,128)}), f32[16,256,64]{1,2,0:T(8,128)}) %all-gather.8.cloned.1.call-update) | async-done | bytes 1048592 | tf_op jit(solution)/shard_map/all_gather | solution.py:35
  298.1 12.4 %all_gather.48 = f32[4,256,64]{1,2,0:T(8,128)S(1)} all-gather(f32[1,256,64]{1,2,0:T(8,128)S(1)} %get-tuple-element.19), channel_id=1, replica_groups=mesh['tm_0'=4,'tm_1'=16,'tm_2'=2,'space'=4] {'tm_0'}, dimensions={0}, use_global_device_ids=true | all-gather | bytes 327680 | tf_op jit(solution)/shard_map/all_gather | solution.py:35
  312.5 2.1 fusion
  315.5 1.5 reshape.2403
  317.1 4.3 %all-to-all-start.1 = ((bf16[4,2,32768]{2,1,0:T(2,128)(2,1)}), bf16[4,2,32768]{2,1,0:T(2,128)(2,1)S(1)}, u32[]{:S(2)}, u32[]{:S(2)}) async-start(bf16[4,2,32768]{2,1,0:T(2,128)(2,1)} %reshape.2403), calls=%async_computation.1 | async-start | bytes 1048576 | tf_op jit(solution)/shard_map/all_to_all | solution.py:163
  321.4 11.0 %all-reduce = (f32[2,4]{1,0:T(2,128)S(1)}, f32[2,4]{1,0:T(2,128)S(1)}, f32[2,4]{1,0:T(2,128)S(1)}) all-reduce(f32[2,4]{1,0:T(2,128)S(1)} %pad_maximum_fusion.5, f32[2,4]{1,0:T(2,128)S(1)} %pad_maximum_fusion.6, f32[2,4]{1,0:T(2,128)S(1)} %pad_maximum_fusion.7), channel_id=1, replica_groups=mesh['tm_0'=4,'tm_1'=16,'tm_2'=2,'space'=4] {'space'}, use_global_device_ids=true, to_apply=%region_2.3 | all-reduce | flops 24 | bytes 192 | tf_op jit(solution)/shard_map/psum | solution.py:168
  335.2 2.3 fusion.59
  (111 shorter events, 21.4 us)
Async XLA Ops:
  12.2 14.4 %all-to-all-start = ((bf16[4,2,34816]{2,1,0:T(2,128)(2,1)}), bf16[4,2,34816]{2,1,0:T(2,128)(2,1)S(1)}, u32[]{:S(2)}, u32[]{:S(2)}) async-start(bf16[4,2,34816]{2,1,0:T(2,128)(2,1)} %reshape.2401), calls=%async_computation | async-start | bytes 1114112 | tf_op jit(solution)/shard_map/all_to_all | solution.py:84
  16.7 102.0 %all-gather.4.cloned.1.call-start = ((), (), s32[]{:S(2)}) async-start(), calls=%async_computation.2 | async-start | bytes 1114112 | tf_op jit(solution)/shard_map/all_gather | solution.py:35
  33.2 11.8 %copy-start.3 = (f32[17,256,64]{1,2,0:T(8,128)}, f32[17,256,64]{1,2,0:T(8,128)S(1)}, u32[]{:S(2)}) copy-start(f32[17,256,64]{1,2,0:T(8,128)S(1)} %convolution_bitcast_fusion) | copy-start | bytes 3342340
  33.3 2.1 copy-start.13
  33.5 11.5 %collective-permute-start = (f32[256,64]{0,1:T(8,128)S(1)}, f32[256,64]{0,1:T(8,128)S(1)}, u32[]{:S(2)}, u32[]{:S(2)}) collective-permute-start(f32[256,64]{0,1:T(8,128)S(1)} %slice_bitcast_fusion.7), channel_id=1, source_target_pairs={{0,4},{4,8},{8,12},{12,16},{16,20},{20,24},{24,28},{28,32},{32,36}... | collective-permute-start | bytes 196616 | tf_op jit(solution)/shard_map/ppermute | solution.py:21
  35.5 9.6 %copy-start.10 = (f32[1,256,64]{1,2,0:T(8,128)}, f32[1,256,64]{1,2,0:T(8,128)S(1)}, u32[]{:S(2)}) copy-start(f32[1,256,64]{1,2,0:T(8,128)S(1)} %bitcast_add_fusion.91) | copy-start | bytes 196612
  49.5 1.6 copy-start.6
  50.2 138.4 %all-gather.6.cloned.1.call-start = ((), (), s32[]{:S(2)}) async-start(), calls=%async_computation.3 | async-start | bytes 1114112 | tf_op jit(solution)/shard_map/all_gather | solution.py:35
  51.0 245.7 %all-gather.8.cloned.1.call-start = ((), (), s32[]{:S(2)}) async-start(), calls=%async_computation.4 | async-start | bytes 1114112 | tf_op jit(solution)/shard_map/all_gather | solution.py:35
  118.7 84.0 %copy-start = (f32[16,256,64]{1,2,0:T(8,128)S(1)}, f32[16,256,64]{1,2,0:T(8,128)}, u32[]{:S(2)}) copy-start(f32[16,256,64]{1,2,0:T(8,128)} %all-gather.4.cloned.1.call-done) | copy-start | bytes 3145732
  190.3 24.8 %copy-start.2 = (f32[16,256,64]{1,2,0:T(8,128)S(1)}, f32[16,256,64]{1,2,0:T(8,128)}, u32[]{:S(2)}) copy-start(f32[16,256,64]{1,2,0:T(8,128)} %all-gather.6.cloned.1.call-done) | copy-start | bytes 3145732
  190.3 24.8 %copy-start.7 = (f32[2,256,64]{1,2,0:T(8,128)S(1)}, f32[2,256,64]{1,2,0:T(8,128)}, u32[]{:S(2)}) copy-start(f32[2,256,64]{1,2,0:T(8,128)} %copy-done.6) | copy-start | bytes 393220
  190.3 24.8 %copy-start.14 = (f32[1,4,256,64]{2,3,1,0:T(8,128)S(1)}, f32[1,4,256,64]{2,3,1,0:T(8,128)}, u32[]{:S(2)}) copy-start(f32[1,4,256,64]{2,3,1,0:T(8,128)} %copy-done.13) | copy-start | bytes 786436
  190.3 24.8 %copy-start.16 = (f32[256,64]{0,1:T(8,128)S(1)}, f32[256,64]{0,1:T(8,128)}, u32[]{:S(2)}) copy-start(f32[256,64]{0,1:T(8,128)} %copy-done.15) | copy-start | bytes 196612
  215.8 11.4 %copy-start.4 = (f32[256,64]{0,1:T(8,128)}, f32[256,64]{0,1:T(8,128)S(1)}, u32[]{:S(2)}) copy-start(f32[256,64]{0,1:T(8,128)S(1)} %get-tuple-element.27) | copy-start | bytes 196612
  218.6 7.7 %collective-permute-start.1 = (f32[256,64]{0,1:T(8,128)S(1)}, f32[256,64]{0,1:T(8,128)S(1)}, u32[]{:S(2)}, u32[]{:S(2)}) collective-permute-start(f32[256,64]{0,1:T(8,128)S(1)} %slice_bitcast_fusion.6), channel_id=1, source_target_pairs={{0,4},{4,8},{8,12},{12,16},{16,20},{20,24},{24,28},{28,32},{32,36}... | collective-permute-start | bytes 196616 | tf_op jit(solution)/shard_map/ppermute | solution.py:21
  227.2 2.8 copy-start.12
  227.3 2.7 copy-start.5
  227.3 2.7 copy-start.17
  230.4 80.2 %copy-start.9 = (f32[4,256,64]{1,2,0:T(8,128)S(1)}, f32[4,256,64]{1,2,0:T(8,128)}, u32[]{:S(2)}) copy-start(f32[4,256,64]{1,2,0:T(8,128)} %copy-done.8) | copy-start | bytes 786436
  296.6 13.9 %copy-start.1 = (f32[16,256,64]{1,2,0:T(8,128)S(1)}, f32[16,256,64]{1,2,0:T(8,128)}, u32[]{:S(2)}) copy-start(f32[16,256,64]{1,2,0:T(8,128)} %all-gather.8.cloned.1.call-done) | copy-start | bytes 3145732
  315.5 5.9 %copy-start.24 = (f32[4]{0:T(128)S(1)}, f32[4]{0:T(128)}, u32[]{:S(2)}) copy-start(f32[4]{0:T(128)} %get-tuple-element.8) | copy-start | bytes 52
  315.5 5.9 %copy-start.23 = (f32[4]{0:T(128)S(1)}, f32[4]{0:T(128)}, u32[]{:S(2)}) copy-start(f32[4]{0:T(128)} %get-tuple-element.40) | copy-start | bytes 52
  317.1 15.9 %all-to-all-start.1 = ((bf16[4,2,32768]{2,1,0:T(2,128)(2,1)}), bf16[4,2,32768]{2,1,0:T(2,128)(2,1)S(1)}, u32[]{:S(2)}, u32[]{:S(2)}) async-start(bf16[4,2,32768]{2,1,0:T(2,128)(2,1)} %reshape.2403), calls=%async_computation.1 | async-start | bytes 1048576 | tf_op jit(solution)/shard_map/all_to_all | solution.py:163
  (8 other events, 6.6 us)
Sparse Core Ops, SparseCore 0:
  50.3 68.3 all-gather.3
  120.8 67.7 all-gather.5
  230.1 66.4 all-gather.7
where the time goes:
time: 345 us; the launch traced here: 344 us
  waiting for transfers between devices  229 us (66%)
  blocking collectives  53.8 us (16%)
  local copies, waits for them, and re-layouts  14.9 us (4%)
  between operations  14.3 us (4%)
  starting transfers between devices  12.7 us (4%)
  other arithmetic  11.9 us (3%)
  matrix products  7.08 us (2%)
    all_gather x3, waiting for transfers between devices, carried_in(): pieces = jax.tree.map(lambda part: lax.all_gather(part, axis), running)  204 us
    all_gather x6, blocking collectives, carried_in(): pieces = jax.tree.map(lambda part: lax.all_gather(part, axis), running)  42.8 us
    ppermute x2, waiting for transfers between devices, passed_along(): return lax.ppermute(block, axis, route)  15.2 us
    psum x1, blocking collectives, per_device(): lax.psum((jnp.stack(norm_rows), jnp.stack(corr_rows), jnp.stack(value_row...  11 us
    all_to_all x1, waiting for transfers between devices, per_device(): lax.all_to_all(halved, 'space', split_axis=2, concat_axis=1, tiled=True)  9.71 us
    unnamed x54, local copies, waits for them, and re-layouts  7.29 us
  transfers between devices with their start and end apart: 7, of which 6 were waited for; matrix products, arithmetic and copies ran while one was open for 0% of the time, Pallas kernels for 0%

commit v1 on v0

v1 whole, which is shorter than its diff:
```python
import functools

import jax
import jax.numpy as jnp
import numpy as np
from jax import lax
from jax.experimental import pallas as pl
from jax.experimental.pallas import tpu as pltpu
from jax.sharding import Mesh
from jax.sharding import PartitionSpec as P

DURATION = 0.004
STEPS = 16
ROWS = 32
MESH = pl.DeviceIdType.MESH
TM = ("tm_0", "tm_1", "tm_2")

GAIN, A4, MID, TOP, DIF, KG, GM, W3, C0, F4, GA2, U1, U2, U3, U4, B4 = range(16)


def tables(n, ny):
    w = n // ny
    k = np.arange(1, n + 1)
    full = np.sqrt(2.0 / (n + 1)) * np.sin(np.pi * ((k[:, None] * k[None, :]) % (2 * (n + 1))) / (n + 1))
    full = full.astype(np.float32)
    half = full.astype(jnp.bfloat16)
    low = (full - half.astype(np.float32)).astype(jnp.bfloat16)
    pair = np.zeros((2, n, ny, 2, w), half.dtype)
    for p in range(2):
        pair[p, :, :, p, :] = half.reshape(n, ny, w)
    pair = pair.reshape(2, n, ny * 2 * w)
    mu = 4.0 * (n + 1) ** 2 * np.sin(np.pi * k / (2 * (n + 1))) ** 2
    mu_rows = np.broadcast_to(mu[:, None], (n, 128)).astype(np.float32)
    mu_cols = np.tile(mu.reshape(ny, 1, w), (1, 8, 2)).astype(np.float32)
    back = np.ascontiguousarray(np.swapaxes(pair, 1, 2))
    return pair, back, np.stack([half, low]), mu_rows, mu_cols


def swap(v):
    return pltpu.roll(v, 64, 1)


def kernel(
    dims,
    forcing, start, pair_in, pair_out, table, mu_rows, mu_cols,
    heat, history, change,
    sbuf, rbuf, s0buf, r0buf, src, u0, cf, ab, tt, cbuf, tc, zbuf, hz, cz, xsend, xbuf, esend, ebuf,
    fsend, fbuf, nsend, nbuf, est, phi, plo, obuf, gbuf, stat, stbuf,
    ysend_s, yrecv_s, y0send_s, y0recv_s, dsend_s, drecv_s, nsend_s, nrecv_s, zsend_s, zrecv_s,
    xsend_s, xrecv_s, esend_s, erecv_s, osend_s, orecv_s, tsend_s, trecv_s,
):
    nx, nz, nc, ny, n = dims
    nd = nx * nz * nc
    half_n, zr, slab = n // 2, n // 2 // nz, n // ny
    steps = nd * STEPS
    bf16, f32 = jnp.bfloat16, jnp.float32
    x, z, core = (lax.axis_index(a) for a in TM)
    y = lax.axis_index("space")
    index = (x * nz + z) * nc + core
    after, before = lax.rem(index + 1, nd), lax.rem(index + nd - 1, nd)

    def place(i):
        return {"tm_0": i // (nz * nc), "tm_1": lax.rem(i // nc, nz), "tm_2": lax.rem(i, nc)}

    def ypeer(k):
        return {"space": lax.rem(y + k, ny)}

    partner = {"tm_2": 1 - core}
    first, last = index == 0, index == nd - 1
    zorder = sorted(range(1, nz), key=lambda k: -min(k, nz - k))

    barrier = pltpu.get_barrier_semaphore()

    def hello(device):
        pl.semaphore_signal(barrier, inc=1, device_id=device, device_id_type=MESH)

    for k in zorder:
        hello({"tm_1": lax.rem(z + k, nz)})
    for k in range(1, nx):
        hello({"tm_0": lax.rem(x + k, nx)})
    for k in range(1, ny):
        hello(ypeer(k))
    hello(partner)

    @pl.when(core == 1)
    def _():
        hello(place(after))

    @pl.when(core == 0)
    def _():
        hello(place(before))

    def remote(s, d, ss, rs, device):
        return pltpu.make_async_remote_copy(
            src_ref=s, dst_ref=d, send_sem=ss, recv_sem=rs, device_id=device, device_id_type=MESH
        )

    def yf(h, k):
        to = lax.rem(y + k, ny)
        return remote(sbuf.at[h, to], rbuf.at[h, y], ysend_s.at[h, k], yrecv_s.at[h, k], ypeer(k))

    def yf_from(h, k):
        frm = lax.rem(y + ny - k, ny)
        return remote(sbuf.at[h, frm], rbuf.at[h, frm], ysend_s.at[h, k], yrecv_s.at[h, k], ypeer(k))

    def y0(k):
        to = lax.rem(y + k, ny)
        return remote(s0buf.at[to], r0buf.at[y], y0send_s.at[k], y0recv_s.at[k], ypeer(k))

    def y0_from(k):
        frm = lax.rem(y + ny - k, ny)
        return remote(s0buf.at[frm], r0buf.at[frm], y0send_s.at[k], y0recv_s.at[k], ypeer(k))

    def column_transform(h):
        a = forcing[8 * h : 8 * h + 4].reshape(4 * slab, n)
        b = forcing[8 * h + 4 : 8 * h + 8].reshape(4 * slab, n)
        out = jnp.dot(a, pair_in[0], preferred_element_type=f32)
        out = out + jnp.dot(b, pair_in[1], preferred_element_type=f32)
        out = out.astype(bf16)
        for r in range(ny):
            for j in range(4):
                sbuf[h, r, :, 128 * j : 128 * j + 128] = out[j * slab : (j + 1) * slab, 128 * r : 128 * r + 128]

    column_transform(0)
    pl.semaphore_wait(barrier, (nz - 1) + (nx - 1) + (ny - 1) + 2)
    for k in range(1, ny):
        yf(0, k).start()

    @pl.when(first)
    def _():
        out = jnp.dot(start[...], pair_in[0], preferred_element_type=f32).astype(bf16)
        for r in range(ny):
            s0buf[r] = out[:, 128 * r : 128 * r + 128]
        for k in range(1, ny):
            y0(k).start()

    column_transform(1)
    for k in range(1, ny):
        yf(1, k).start()
    rbuf[0, y] = sbuf[0, y]
    rbuf[1, y] = sbuf[1, y]

    low_lanes = lax.broadcasted_iota(jnp.int32, (ROWS, 128), 1) < 64
    h_step = DURATION / steps
    col = mu_cols[y][0:1, :]

    def coefficients(i, carry):
        rows = pl.ds(pl.multiple_of(i * ROWS, ROWS), ROWS)
        d = h_step * (mu_rows[rows, :] + col)
        g = 1.0 / (1.0 + d)
        m = 1.0 / (1.0 + 4.0 * d)
        top_inv = 1.0 + 16.0 * d
        top = 1.0 / top_inv
        g2 = g * g
        a = g2 * g2
        m2 = m * m
        m3 = m2 * m
        e = 4.0 * d
        dif = -(d * d) * (6.0 + d * (4.0 + d)) * a * m
        gm_top = e * e * (6.0 + e * (4.0 + e)) * (m2 * m2)
        gm = gm_top * top
        kg = dif * m3 * top_inv - gm_top
        w3 = m3 * a * top_inv
        f4 = dif * m2 * a - kg * m3 * a
        c0 = m3 * a * kg + 3.0 * a * dif * m2
        c3 = 2.0 * m * a * a * dif - c0 * w3
        ga2 = a * (dif - kg * m)
        b4 = c3 * top_inv + w3 * f4 * top_inv
        b1 = w3 * m * ga2 + a * a * dif
        b2 = w3 * ga2
        b3 = -w3 * kg * a
        cf[GAIN, rows, :] = g
        cf[A4, rows, :] = a
        cf[MID, rows, :] = m
        cf[TOP, rows, :] = top
        cf[DIF, rows, :] = dif
        cf[KG, rows, :] = kg
        cf[GM, rows, :] = gm
        cf[W3, rows, :] = w3
        cf[C0, rows, :] = jnp.where(low_lanes, 0.0, c0)
        cf[F4, rows, :] = f4
        cf[GA2, rows, :] = ga2
        cf[U1, rows, :] = jnp.where(low_lanes, a * m2, b2)
        cf[U2, rows, :] = jnp.where(low_lanes, a * m, b1)
        cf[U3, rows, :] = jnp.where(low_lanes, a, b4)
        cf[U4, rows, :] = jnp.where(low_lanes, w3, b3)
        cf[B4, rows, :] = b4
        return carry

    lax.fori_loop(0, n // ROWS, coefficients, 0)

    mine = pl.ds(pl.multiple_of(core * half_n + z * zr, zr), zr)
    top_own, c0_own = cf[TOP, mine, :], cf[C0, mine, :]
    chip_gain, chip_mix = top_own * top_own, 2.0 * c0_own * top_own
    power, mix = jnp.ones_like(chip_gain), jnp.zeros_like(chip_gain)
    for k in range(nz + 1):
        hz[k] = power
        cz[k] = mix
        power, mix = power * chip_gain, mix * chip_gain + power * chip_mix

    u0[...] = jnp.zeros_like(u0)

    @pl.when(first)
    def _():
        for k in range(1, ny):
            y0_from(k).wait_recv()
        r0buf[y] = s0buf[y]
        u0[...] = jnp.dot(table[0], r0buf[...].reshape(n, 128), preferred_element_type=f32)

    for h in range(2):
        for k in range(1, ny):
            yf_from(h, k).wait_recv()
        src[h] = jnp.dot(table[0], rbuf[h].reshape(n, 512), preferred_element_type=f32)

    def relax(i, carry):
        rows = pl.ds(pl.multiple_of(i * ROWS, ROWS), ROWS)
        g = cf[GAIN, rows, :]
        ends = []
        for h in range(2):
            v = None
            for j in range(4):
                s = g * src[h, rows, 128 * j : 128 * j + 128]
                src[h, rows, 128 * j : 128 * j + 128] = s
                v = s if v is None else g * v + s
            ends.append(v)
        va, vb = ends
        va = va + cf[A4, rows, :] * u0[rows, :]
        ab[0, rows, :] = va
        ab[1, rows, :] = vb
        tt[rows, :] = (
            cf[U1, rows, :] * va + cf[U2, rows, :] * swap(va) + cf[U3, rows, :] * vb + cf[U4, rows, :] * swap(vb)
        )
        return carry

    lax.fori_loop(0, n // ROWS, relax, 0)

    own = pl.ds(pl.multiple_of(core * half_n, half_n), half_n)
    other = pl.ds(pl.multiple_of((1 - core) * half_n, half_n), half_n)
    join = remote(tt.at[other], cbuf, dsend_s.at[0], drecv_s.at[0], partner)
    join.start()

    wide = lax.broadcasted_iota(jnp.int32, (half_n, 128), 1) < 64
    nsend[0] = jnp.where(wide, swap(ab[1, 0:half_n, :]), ab[1, half_n:n, :])

    def pass_on(k):
        return remote(nsend.at[k], nbuf.at[k], nsend_s.at[k], nrecv_s.at[k], place(after))

    @pl.when(jnp.logical_not(last))
    def _():
        pass_on(0).start()

    @pl.when(first)
    def _():
        nbuf[...] = jnp.zeros_like(nbuf)

    join.wait_recv()
    own_t, got_t = tt[own, :], cbuf[...]
    early = jnp.where(core == 0, own_t, got_t)
    late = jnp.where(core == 0, got_t, own_t)
    top_half, c0_half = cf[TOP, own, :], cf[C0, own, :]
    joined = top_half * early + c0_half * swap(early) + late
    tc[...] = joined.reshape(nz, zr, 128)

    def zs(k):
        to = lax.rem(z + k, nz)
        return remote(tc.at[to], zbuf.at[z], zsend_s.at[k], zrecv_s.at[k], {"tm_1": to})

    def zs_from(k):
        frm = lax.rem(z + nz - k, nz)
        return remote(tc.at[frm], zbuf.at[frm], zsend_s.at[k], zrecv_s.at[k], {"tm_1": frm})

    for k in zorder:
        zs(k).start()
    zbuf[z] = tc[z]

    @pl.when(jnp.logical_not(first))
    def _():
        pass_on(0).wait_recv()

    def unpack(k, i, rows):
        v = nbuf[k, pl.ds(pl.multiple_of(lax.rem(i, n // ROWS // 2) * ROWS, ROWS), ROWS), :]
        return jnp.where(i < n // ROWS // 2, v, swap(v))

    def follow(i, carry):
        rows = pl.ds(pl.multiple_of(i * ROWS, ROWS), ROWS)
        top_rows = pl.ds(pl.multiple_of(half_n + i * ROWS, ROWS), ROWS)
        v = nbuf[0, rows, :]

        def part(r, b4p):
            va, vb = ab[0, r, :], ab[1, r, :]
            ga2 = cf[GA2, r, :]
            out = cf[F4, r, :] * b4p + cf[MID, r, :] * ga2 * va + ga2 * swap(va)
            return out - cf[KG, r, :] * cf[A4, r, :] * vb

        nsend[1, rows, :] = jnp.where(low_lanes, part(rows, v), swap(part(top_rows, swap(v))))
        return carry

    lax.fori_loop(0, n // ROWS // 2, follow, 0)

    @pl.when(jnp.logical_not(last))
    def _():
        pass_on(1).start()

    for k in range(1, nz):
        zs_from(k).wait_recv()

    local, states = jnp.zeros_like(chip_gain), []
    for k in range(nz):
        states.append(local)
        local = chip_gain * local + zbuf[k]
    total = local
    mixed, mixes = jnp.zeros_like(chip_gain), []
    for k in range(nz):
        mixes.append(mixed)
        mixed = chip_gain * mixed + chip_mix * swap(states[k])
    xsend[...] = total + mixed
    for k in range(nz):
        esend[k] = states[k] + mixes[k]

    def xs(k):
        return remote(xsend, xbuf.at[x], xsend_s.at[k], xrecv_s.at[k], {"tm_0": lax.rem(x + k, nx)})

    def xs_from(k):
        frm = lax.rem(x + nx - k, nx)
        return remote(xsend, xbuf.at[frm], xsend_s.at[k], xrecv_s.at[k], {"tm_0": frm})

    for k in range(1, nx):
        xs(k).start()
    for k in range(1, nx):
        xs_from(k).wait_recv()
    entering = jnp.zeros_like(chip_gain)
    for k in range(nx - 1):
        stepped = hz[nz] * entering + cz[nz] * swap(entering) + xbuf[k]
        entering = jnp.where(k < x, stepped, entering)
    turned = swap(entering)
    for k in range(nz):
        esend[k] = esend[k] + hz[k] * entering + cz[k] * turned

    def es(k):
        to = lax.rem(z + k, nz)
        return remote(esend.at[to], ebuf.at[z], esend_s.at[k], erecv_s.at[k], {"tm_1": to})

    def es_from(k):
        frm = lax.rem(z + nz - k, nz)
        return remote(esend.at[frm], ebuf.at[frm], esend_s.at[k], erecv_s.at[k], {"tm_1": frm})

    for k in zorder:
        es(k).start()
    ebuf[z] = esend[z]
    for k in range(1, nz):
        es_from(k).wait_recv()

    chip = ebuf[...].reshape(half_n, 128)
    second = cf[TOP, own, :] * chip + cf[C0, own, :] * swap(chip) + jnp.where(core == 0, tt[own, :], cbuf[...])
    fsend[...] = jnp.where(core == 0, second, chip)
    est[own, :] = jnp.where(core == 0, chip, second)
    give = remote(fsend, fbuf, dsend_s.at[1], drecv_s.at[1], partner)
    give.start()
    give.wait_recv()
    est[other, :] = fbuf[...]

    @pl.when(jnp.logical_not(first))
    def _():
        pass_on(1).wait_recv()

    def entries(i, rows):
        b4p, bkp = unpack(0, i, rows), unpack(1, i, rows)
        v = est[rows, :]
        e1 = v - cf[W3, rows, :] * b4p
        e2 = swap(v) - cf[W3, rows, :] * bkp - cf[B4, rows, :] * b4p
        return b4p, e1, e2, cf[KG, rows, :] * e1 + bkp

    def iterations(i, rows):
        a, m, top = cf[A4, rows, :], cf[MID, rows, :], cf[TOP, rows, :]
        dif, gm = cf[DIF, rows, :], cf[GM, rows, :]
        b4p, e1, e2, d4p = entries(i, rows)
        va, vb = ab[0, rows, :], ab[1, rows, :]
        b = [va, swap(va), vb, swap(vb)]
        r1 = [a * b4p, a * b[0], a * b[1], a * b[2]]

        def correct(entry, r):
            p1 = m * entry + r[0]
            p2 = m * p1 + r[1]
            p3 = m * p2 + r[2]
            q = m * (m * (m * r[0] + r[1]) + r[2]) + r[3]
            return [p1, p2, p3, top * entry + q]

        k1 = correct(e1, r1)
        v1 = [b[c] + k1[c] for c in range(4)]
        d = [dif * e1, dif * k1[0], dif * k1[1], dif * k1[2] - gm * e1]
        r2 = [a * d4p, a * d[0], a * d[1], a * d[2]]
        k2 = correct(e2, r2)
        v2 = [v1[c] + d[c] + k2[c] for c in range(4)]
        v0 = b4p + e1 + d4p + e2
        return r1, k1, v1, r2, k2, v2, v0

    def path(i, carry):
        rows = pl.ds(pl.multiple_of(i * ROWS, ROWS), ROWS)
        _, _, _, _, _, v2, v0 = iterations(i, rows)
        v0 = jnp.where(first, u0[rows, :], v0)
        g = cf[GAIN, rows, :]
        points = [v0] + v2
        for h in range(2):
            at = jnp.where(low_lanes, points[2 * h], swap(points[2 * h + 1]))
            end = jnp.where(low_lanes, points[2 * h + 1], swap(points[2 * h + 2]))
            for j in range(4):
                lanes = slice(128 * j, 128 * j + 128)
                at = g * at + src[h, rows, lanes] if j < 3 else end
                high = at.astype(bf16)
                phi[h, rows, lanes] = high
                plo[h, rows, lanes] = (at - high.astype(f32)).astype(bf16)
        return carry

    lax.fori_loop(0, n // ROWS, path, 0)

    def og(h, k):
        to = lax.rem(y + k, ny)
        return remote(obuf.at[h, to], gbuf.at[h, y], osend_s.at[h, k], orecv_s.at[h, k], ypeer(k))

    def og_from(h, k):
        frm = lax.rem(y + ny - k, ny)
        return remote(obuf.at[h, frm], gbuf.at[h, frm], osend_s.at[h, k], orecv_s.at[h, k], ypeer(k))

    for h in range(2):
        out = jnp.dot(table[0], phi[h], preferred_element_type=f32)
        out = out + jnp.dot(table[0], plo[h], preferred_element_type=f32)
        out = out + jnp.dot(table[1], phi[h], preferred_element_type=f32)
        obuf[h] = out.astype(bf16).reshape(ny, slab, 512)
        for k in range(1, ny):
            og(h, k).start()
    gbuf[0, y] = obuf[0, y]
    gbuf[1, y] = obuf[1, y]

    stat[...] = jnp.zeros_like(stat)

    def norms(i, carry):
        rows = pl.ds(pl.multiple_of(i * ROWS, ROWS), ROWS)
        r1, k1, v1, r2, k2, v2, _ = iterations(i, rows)
        for group, fields in enumerate((r1, r2, k1, k2, v1, v2)):
            for c in range(4):
                at = 4 * group + c
                sq = fields[c] * fields[c]
                stat[at : at + 1, :] = stat[at : at + 1, :] + jnp.sum(sq, axis=0, keepdims=True)
        return carry

    lax.fori_loop(0, n // ROWS, norms, 0)

    def ts(k):
        return remote(stat, stbuf.at[y], tsend_s.at[k], trecv_s.at[k], ypeer(k))

    def ts_from(k):
        frm = lax.rem(y + ny - k, ny)
        return remote(stat, stbuf.at[frm], tsend_s.at[k], trecv_s.at[k], ypeer(k))

    for k in range(1, ny):
        ts(k).start()
    stbuf[y] = stat[...]

    for h in range(2):
        for k in range(1, ny):
            og_from(h, k).wait_recv()
        for p in range(2):
            lhs = jnp.concatenate(
                [
                    jnp.concatenate([gbuf[h, s, :, 128 * j : 128 * j + 128] for s in range(ny)], axis=1)
                    for j in range(4)
                ],
                axis=0,
            )
            out = jnp.dot(lhs, pair_out[p], preferred_element_type=f32)
            for j in range(4):
                heat[8 * h + 4 * p + j] = out[j * slab : (j + 1) * slab, :]

    for k in range(1, ny):
        ts_from(k).wait_recv()
    sums = stbuf[0]
    for s in range(1, ny):
        sums = sums + stbuf[s]
    keep = lax.broadcasted_iota(jnp.int32, sums.shape, 1) < 64
    sums = jnp.sum(jnp.where(keep, sums, 0.0), axis=1, keepdims=True)
    residual = jnp.broadcast_to(jnp.sqrt(sums[0:8] / (n * n)), (8, 128))
    moved = jnp.broadcast_to(jnp.sqrt(sums[8:16] / sums[16:24]), (8, 128))
    spot = lax.broadcasted_iota(jnp.int32, (8, 128), 1) == lax.rem(lax.broadcasted_iota(jnp.int32, (8, 128), 0), 4)
    for ref, v in ((history, residual), (change, moved)):
        v = jnp.where(spot, v, 0.0)
        for it in range(2):
            ref[it : it + 1, :] = jnp.sum(v[4 * it : 4 * it + 4], axis=0, keepdims=True)[:, 0:4]

    for k in range(1, ny):
        for h in range(2):
            yf(h, k).wait_send()
            og(h, k).wait_send()
        ts(k).wait_send()

    @pl.when(first)
    def _():
        for k in range(1, ny):
            y0(k).wait_send()

    join.wait_send()
    give.wait_send()

    @pl.when(jnp.logical_not(last))
    def _():
        pass_on(0).wait_send()
        pass_on(1).wait_send()

    for k in range(1, nz):
        zs(k).wait_send()
        es(k).wait_send()
    for k in range(1, nx):
        xs(k).wait_send()


def per_device(dims, forcing, starting_heat):
    nx, nz, nc, ny, n = dims
    slab, half_n, zr = n // ny, n // 2, n // 2 // nz
    bf16, f32 = jnp.bfloat16, jnp.float32
    consts = tables(n, ny)
    dma = pltpu.SemaphoreType.DMA
    scratch = [
        ((2, ny, slab, 512), bf16),
        ((2, ny, slab, 512), bf16),
        ((ny, slab, 128), bf16),
        ((ny, slab, 128), bf16),
        ((2, n, 512), f32),
        ((n, 128), f32),
        ((16, n, 128), f32),
        ((2, n, 128), f32),
        ((n, 128), f32),
        ((half_n, 128), f32),
        ((nz, zr, 128), f32),
        ((nz, zr, 128), f32),
        ((nz + 1, zr, 128), f32),
        ((nz + 1, zr, 128), f32),
        ((zr, 128), f32),
        ((nx, zr, 128), f32),
        ((nz, zr, 128), f32),
        ((nz, zr, 128), f32),
        ((half_n, 128), f32),
        ((half_n, 128), f32),
        ((2, half_n, 128), f32),
        ((2, half_n, 128), f32),
        ((n, 128), f32),
        ((2, n, 512), bf16),
        ((2, n, 512), bf16),
        ((2, ny, slab, 512), bf16),
        ((2, ny, slab, 512), bf16),
        ((24, 128), f32),
        ((ny, 24, 128), f32),
    ]
    sems = [
        (2, ny), (2, ny), (ny,), (ny,), (2,), (2,), (2,), (2,), (nz,), (nz,),
        (nx,), (nx,), (nz,), (nz,), (2, ny), (2, ny), (ny,), (ny,),
    ]
    vmem = pl.BlockSpec(memory_space=pltpu.VMEM)
    return pl.pallas_call(
        functools.partial(kernel, dims),
        out_shape=(
            jax.ShapeDtypeStruct((STEPS, slab, n), f32),
            jax.ShapeDtypeStruct((2, 4), f32),
            jax.ShapeDtypeStruct((2, 4), f32),
        ),
        in_specs=[vmem] * 7,
        out_specs=(vmem, vmem, vmem),
        scratch_shapes=[pltpu.VMEM(s, d) for s, d in scratch] + [dma(s) for s in sems],
        compiler_params=pltpu.CompilerParams(
            collective_id=0, has_side_effects=True, vmem_limit_bytes=48 * 1024 * 1024
        ),
    )(forcing, starting_heat, *[jnp.asarray(c) for c in consts])


def build(mesh, nx, nz, nc, n):
    ny = mesh.shape["space"]
    torus = Mesh(mesh.devices.reshape(nx, nz, nc, ny), TM + ("space",))
    return jax.shard_map(
        functools.partial(per_device, (nx, nz, nc, ny, n)),
        mesh=torus,
        in_specs=(P(TM, "space", None), P("space", None)),
        out_specs=(P(TM, "space", None), P(None, TM), P(None, TM)),
        check_vma=False,
    )


def solution(mesh):
    return build(mesh, 4, 16, 2, 256)
```

time: 345 us -> 67.4 us (0.20)
  the two profiles are of different devices: /device:TPU:2 before, /device:TPU:1 now
where the time goes in v1:
time: 67.4 us; the launch traced here: 67 us
  Pallas kernels  57.8 us (86%)
  local copies, waits for them, and re-layouts  8.54 us (13%)
    pallas_call x1, Pallas kernels, per_device(): pl.pallas_call(functools.partial(kernel, dims), out_shape=(jax.ShapeDtype...  57.8 us
    unnamed x17, local copies, waits for them, and re-layouts  8.54 us

profile of v1, /device:TPU:1, one launch (start us, length us, event | category | flops | bytes accessed | tf_op | source)
XLA Modules:
  0.0 67.0 jit_solution(5463041616145363017)
XLA Ops:
  0.6 0.0 copy-start
  0.6 1.0 %copy-done = bf16[16,64,256]{2,1,0:T(8,128)(2,1)S(1)} copy-done((bf16[16,64,256]{2,1,0:T(8,128)(2,1)S(1)}, bf16[16,64,256]{2,1,0:T(8,128)(2,1)}, u32[]{:S(2)}) %copy-start) | copy-done | bytes 524312
  1.7 0.0 copy-start.1
  1.7 1.0 %copy-done.1 = bf16[2,512,256]{2,1,0:T(8,128)(2,1)S(1)} copy-done((bf16[2,512,256]{2,1,0:T(8,128)(2,1)S(1)}, bf16[2,512,256]{2,1,0:T(8,128)(2,1)}, u32[]{:S(2)}) %copy-start.1) | copy-done | bytes 524312
  2.7 0.0 copy-start.2
  2.7 1.0 %copy-done.2 = bf16[2,256,512]{2,1,0:T(8,128)(2,1)S(1)} copy-done((bf16[2,256,512]{2,1,0:T(8,128)(2,1)S(1)}, bf16[2,256,512]{2,1,0:T(8,128)(2,1)}, u32[]{:S(2)}) %copy-start.2) | copy-done | bytes 524312
  3.8 0.0 copy-start.3
  3.8 0.9 %copy-done.3 = bf16[2,256,256]{2,1,0:T(8,128)(2,1)S(1)} copy-done((bf16[2,256,256]{2,1,0:T(8,128)(2,1)S(1)}, bf16[2,256,256]{2,1,0:T(8,128)(2,1)}, u32[]{:S(2)}) %copy-start.3) | copy-done | bytes 262168
  4.7 0.0 copy-start.4
  4.7 0.9 %copy-done.4 = f32[256,128]{1,0:T(8,128)S(1)} copy-done((f32[256,128]{1,0:T(8,128)S(1)}, f32[256,128]{1,0:T(8,128)}, u32[]{:S(2)}) %copy-start.4) | copy-done | bytes 131096
  5.6 0.0 copy-start.5
  5.6 0.8 %copy-done.5 = bf16[64,256]{1,0:T(8,128)(2,1)S(1)} copy-done((bf16[64,256]{1,0:T(8,128)(2,1)S(1)}, bf16[64,256]{1,0:T(8,128)(2,1)}, u32[]{:S(2)}) %copy-start.5) | copy-done | bytes 32792
  6.4 0.0 copy-start.6
  6.4 0.7 %copy-done.6 = f32[4,8,128]{2,1,0:T(8,128)S(1)} copy-done((f32[4,8,128]{2,1,0:T(8,128)S(1)}, f32[4,8,128]{2,1,0:T(8,128)}, u32[]{:S(2)}) %copy-start.6) | copy-done | bytes 16408
  7.1 57.8 %shard_map.94 = (f32[16,64,256]{2,1,0:T(8,128)S(1)}, f32[2,4]{1,0:T(2,128)S(1)}, f32[2,4]{1,0:T(2,128)S(1)}) custom-call(bf16[16,64,256]{2,1,0:T(8,128)(2,1)S(1)} %copy-done, bf16[64,256]{1,0:T(8,128)(2,1)S(1)} %copy-done.5, bf16[2,256,512]{2,1,0:T(8,128)(2,1)S(1)} %copy-done.2, bf16[2,512,256]{2,1,0:T(8,128)(2,1)S(1)} %copy-done.1, ...), custom_call_target="tpu_custom_call" | custom-call | tf_op jit(solution)/shard_map/pallas_call | solution.py:557
  64.9 1.0 %copy.13 = f32[16,64,256]{2,1,0:T(8,128)} copy(f32[16,64,256]{2,1,0:T(8,128)S(1)} %get-tuple-element.6) | data formatting | bytes 2097152
  65.9 0.6 copy.14
  66.4 0.6 copy.15
Async XLA Ops:
  0.6 1.0 %copy-start = (bf16[16,64,256]{2,1,0:T(8,128)(2,1)S(1)}, bf16[16,64,256]{2,1,0:T(8,128)(2,1)}, u32[]{:S(2)}) copy-start(bf16[16,64,256]{2,1,0:T(8,128)(2,1)} %forcing.1) | copy-start | bytes 1572868
  1.7 1.0 %copy-start.1 = (bf16[2,512,256]{2,1,0:T(8,128)(2,1)S(1)}, bf16[2,512,256]{2,1,0:T(8,128)(2,1)}, u32[]{:S(2)}) copy-start(bf16[2,512,256]{2,1,0:T(8,128)(2,1)} %constant.11.clone.pair_out) | copy-start | bytes 1572868
  2.7 1.0 %copy-start.2 = (bf16[2,256,512]{2,1,0:T(8,128)(2,1)S(1)}, bf16[2,256,512]{2,1,0:T(8,128)(2,1)}, u32[]{:S(2)}) copy-start(bf16[2,256,512]{2,1,0:T(8,128)(2,1)} %constant.10.clone.pair_in) | copy-start | bytes 1572868
  3.8 0.9 %copy-start.3 = (bf16[2,256,256]{2,1,0:T(8,128)(2,1)S(1)}, bf16[2,256,256]{2,1,0:T(8,128)(2,1)}, u32[]{:S(2)}) copy-start(bf16[2,256,256]{2,1,0:T(8,128)(2,1)} %constant.12.clone.table) | copy-start | bytes 786436
  4.7 0.9 %copy-start.4 = (f32[256,128]{1,0:T(8,128)S(1)}, f32[256,128]{1,0:T(8,128)}, u32[]{:S(2)}) copy-start(f32[256,128]{1,0:T(8,128)} %constant.13.clone.mu_rows) | copy-start | bytes 393220
  5.6 0.8 %copy-start.5 = (bf16[64,256]{1,0:T(8,128)(2,1)S(1)}, bf16[64,256]{1,0:T(8,128)(2,1)}, u32[]{:S(2)}) copy-start(bf16[64,256]{1,0:T(8,128)(2,1)} %start.1) | copy-start | bytes 98308
  6.4 0.7 %copy-start.6 = (f32[4,8,128]{2,1,0:T(8,128)S(1)}, f32[4,8,128]{2,1,0:T(8,128)}, u32[]{:S(2)}) copy-start(f32[4,8,128]{2,1,0:T(8,128)} %constant.14.clone.mu_cols) | copy-start | bytes 49156

commit v2 on v1

--- a/solution.py
+++ b/solution.py
@@ -12,6 +12,7 @@
 DURATION = 0.004
 STEPS = 16
 ROWS = 32
+VMEM_GRANT = 62 * 1024 * 1024
 MESH = pl.DeviceIdType.MESH
 TM = ("tm_0", "tm_1", "tm_2")
 
@@ -42,12 +43,12 @@
 
 def kernel(
     dims,
-    forcing, start, pair_in, pair_out, table, mu_rows, mu_cols,
+    forcing_h, start_h, pair_in_h, pair_out_h, table_h, mu_rows_h, mu_cols_h,
     heat, history, change,
-    sbuf, rbuf, s0buf, r0buf, src, u0, cf, ab, tt, cbuf, tc, zbuf, hz, cz, xsend, xbuf, esend, ebuf,
+    forcing, start, pair_in, pair_out, table, mu_rows, mu_cols, sbuf, rbuf, s0buf, r0buf, src, u0, cf, ab, tt, cbuf, tc, zbuf, hz, cz, xsend, xbuf, esend, ebuf,
     fsend, fbuf, nsend, nbuf, est, phi, plo, obuf, gbuf, stat, stbuf,
     ysend_s, yrecv_s, y0send_s, y0recv_s, dsend_s, drecv_s, nsend_s, nrecv_s, zsend_s, zrecv_s,
-    xsend_s, xrecv_s, esend_s, erecv_s, osend_s, orecv_s, tsend_s, trecv_s,
+    xsend_s, xrecv_s, esend_s, erecv_s, osend_s, orecv_s, tsend_s, trecv_s, load_s,
 ):
     nx, nz, nc, ny, n = dims
     nd = nx * nz * nc
@@ -69,6 +70,12 @@
     first, last = index == 0, index == nd - 1
     zorder = sorted(range(1, nz), key=lambda k: -min(k, nz - k))
 
+    sources = (pair_in_h, forcing_h, start_h, mu_cols_h, mu_rows_h, table_h, pair_out_h)
+    targets = (pair_in, forcing, start, mu_cols, mu_rows, table, pair_out)
+    loads = [pltpu.make_async_copy(a, b, load_s.at[i]) for i, (a, b) in enumerate(zip(sources, targets))]
+    for load in loads:
+        load.start()
+
     barrier = pltpu.get_barrier_semaphore()
 
     def hello(device):
@@ -121,6 +128,8 @@
             for j in range(4):
                 sbuf[h, r, :, 128 * j : 128 * j + 128] = out[j * slab : (j + 1) * slab, 128 * r : 128 * r + 128]
 
+    for load in loads[:2]:
+        load.wait()
     column_transform(0)
     pl.semaphore_wait(barrier, (nz - 1) + (nx - 1) + (ny - 1) + 2)
     for k in range(1, ny):
@@ -128,6 +137,7 @@
 
     @pl.when(first)
     def _():
+        loads[2].wait()
         out = jnp.dot(start[...], pair_in[0], preferred_element_type=f32).astype(bf16)
         for r in range(ny):
             s0buf[r] = out[:, 128 * r : 128 * r + 128]
@@ -139,6 +149,13 @@
         yf(1, k).start()
     rbuf[0, y] = sbuf[0, y]
     rbuf[1, y] = sbuf[1, y]
+
+    @pl.when(jnp.logical_not(first))
+    def _():
+        loads[2].wait()
+
+    for load in loads[3:]:
+        load.wait()
 
     low_lanes = lax.broadcasted_iota(jnp.int32, (ROWS, 128), 1) < 64
     h_step = DURATION / steps
@@ -512,6 +529,15 @@
         xs(k).wait_send()
 
 
+def store(heat_v, history_v, change_v, heat, history, change, sems):
+    pairs = ((heat_v, heat), (history_v, history), (change_v, change))
+    copies = [pltpu.make_async_copy(a, b, sems.at[i]) for i, (a, b) in enumerate(pairs)]
+    for copy in copies:
+        copy.start()
+    for copy in copies:
+        copy.wait()
+
+
 def per_device(dims, forcing, starting_heat):
     nx, nz, nc, ny, n = dims
     slab, half_n, zr = n // ny, n // 2, n // 2 // nz
@@ -519,6 +545,11 @@
     consts = tables(n, ny)
     dma = pltpu.SemaphoreType.DMA
     scratch = [
+        ((STEPS, slab, n), bf16),
+        ((slab, n), bf16),
+    ]
+    scratch += [(c.shape, c.dtype) for c in consts]
+    scratch += [
         ((2, ny, slab, 512), bf16),
         ((2, ny, slab, 512), bf16),
         ((ny, slab, 128), bf16),
@@ -551,23 +582,29 @@
     ]
     sems = [
         (2, ny), (2, ny), (ny,), (ny,), (2,), (2,), (2,), (2,), (nz,), (nz,),
-        (nx,), (nx,), (nz,), (nz,), (2, ny), (2, ny), (ny,), (ny,),
+        (nx,), (nx,), (nz,), (nz,), (2, ny), (2, ny), (ny,), (ny,), (7,),
     ]
     vmem = pl.BlockSpec(memory_space=pltpu.VMEM)
-    return pl.pallas_call(
+    hbm = pl.BlockSpec(memory_space=pltpu.HBM)
+    shapes = ((STEPS, slab, n), (2, 4), (2, 4))
+    held = pl.pallas_call(
         functools.partial(kernel, dims),
-        out_shape=(
-            jax.ShapeDtypeStruct((STEPS, slab, n), f32),
-            jax.ShapeDtypeStruct((2, 4), f32),
-            jax.ShapeDtypeStruct((2, 4), f32),
-        ),
-        in_specs=[vmem] * 7,
+        out_shape=tuple(pltpu.VMEM(s, f32) for s in shapes),
+        in_specs=[hbm] * 7,
         out_specs=(vmem, vmem, vmem),
         scratch_shapes=[pltpu.VMEM(s, d) for s, d in scratch] + [dma(s) for s in sems],
         compiler_params=pltpu.CompilerParams(
-            collective_id=0, has_side_effects=True, vmem_limit_bytes=48 * 1024 * 1024
+            collective_id=0, has_side_effects=True, vmem_limit_bytes=VMEM_GRANT
         ),
     )(forcing, starting_heat, *[jnp.asarray(c) for c in consts])
+    return pl.pallas_call(
+        store,
+        out_shape=tuple(jax.ShapeDtypeStruct(s, f32) for s in shapes),
+        in_specs=[vmem] * 3,
+        out_specs=(hbm, hbm, hbm),
+        scratch_shapes=[dma((3,))],
+        compiler_params=pltpu.CompilerParams(vmem_limit_bytes=4 * 1024 * 1024),
+    )(*held)
 
 
 def build(mesh, nx, nz, nc, n):

time: 67.4 us -> 59.2 us (0.88)
  local copies, waits for them, and re-layouts: 8.54 us -> 0 us
    unnamed x17 -> x0, local copies, waits for them, and re-layouts: 8.54 us -> none
    pallas_call x1 -> x2, Pallas kernels: 57.8 us -> 58.4 us  [the longest x1 57.4 us: per_device(): pl.pallas_call(functools.partial(kernel, dims), out_shape=tuple((pltpu.VM...]
where the time goes in v2:
time: 59.2 us; the launch traced here: 59 us
  Pallas kernels  58.4 us (99%)
  between operations  0.64 us (1%)
    pallas_call x1, Pallas kernels, per_device(): pl.pallas_call(functools.partial(kernel, dims), out_shape=tuple((pltpu.VM...  57.4 us

profile of v2, /device:TPU:1, one launch (start us, length us, event | category | flops | bytes accessed | tf_op | source)
XLA Modules:
  0.0 59.0 jit_solution(11559454217034070073)
XLA Ops:
  0.6 57.4 %shard_map.94 = (f32[16,64,256]{2,1,0:T(8,128)S(1)}, f32[2,4]{1,0:T(2,128)S(1)}, f32[2,4]{1,0:T(2,128)S(1)}) custom-call(bf16[16,64,256]{2,1,0:T(8,128)(2,1)} %forcing_h.1, bf16[64,256]{1,0:T(8,128)(2,1)} %start_h.1, bf16[2,256,512]{2,1,0:T(8,128)(2,1)} %constant.10.clone.pair_in_h, bf16[2,512,256]{2,1,0:T(8,128)(2,1)} %constant.11.clone.pair_out_h, ...), custom_call_target="tpu_custom_call" | custom-call | tf_op jit(solution)/shard_map/pallas_call | solution.py:590
  58.0 1.0 %shard_map.95 = (f32[16,64,256]{2,1,0:T(8,128)}, f32[2,4]{1,0:T(2,128)}, f32[2,4]{1,0:T(2,128)}) custom-call(f32[16,64,256]{2,1,0:T(8,128)S(1)} %get-tuple-element.6.heat_v, f32[2,4]{1,0:T(2,128)S(1)} %get-tuple-element.7.history_v, f32[2,4]{1,0:T(2,128)S(1)} %get-tuple-element.8.change_v), custom_call_target="tpu_custom_call" | custom-call | tf_op jit(solution)/shard_map/pallas_call | solution.py:600

commit v3 on v2

--- a/solution.py
+++ b/solution.py
@@ -45,10 +45,10 @@
     dims,
     forcing_h, start_h, pair_in_h, pair_out_h, table_h, mu_rows_h, mu_cols_h,
     heat, history, change,
-    forcing, start, pair_in, pair_out, table, mu_rows, mu_cols, sbuf, rbuf, s0buf, r0buf, src, u0, cf, ab, tt, cbuf, tc, zbuf, hz, cz, xsend, xbuf, esend, ebuf,
+    forcing, start, pair_in, pair_out, table, mu_rows, mu_cols, sbuf, rbuf, s0buf, r0buf, src, xc, yc, u0, cf, ab, tt, cbuf, tc, zbuf, hz, cz, xsend, xbuf, esend, ebuf,
     fsend, fbuf, nsend, nbuf, est, phi, plo, obuf, gbuf, stat, stbuf,
     ysend_s, yrecv_s, y0send_s, y0recv_s, dsend_s, drecv_s, nsend_s, nrecv_s, zsend_s, zrecv_s,
-    xsend_s, xrecv_s, esend_s, erecv_s, osend_s, orecv_s, tsend_s, trecv_s, load_s,
+    xsend_s, xrecv_s, esend_s, erecv_s, osend_s, orecv_s, tsend_s, trecv_s, load_s, known_s,
 ):
     nx, nz, nc, ny, n = dims
     nd = nx * nz * nc
@@ -68,12 +68,13 @@
 
     partner = {"tm_2": 1 - core}
     first, last = index == 0, index == nd - 1
+    yorder = sorted(range(1, ny), key=lambda k: -min(k, ny - k))
     zorder = sorted(range(1, nz), key=lambda k: -min(k, nz - k))
 
     sources = (pair_in_h, forcing_h, start_h, mu_cols_h, mu_rows_h, table_h, pair_out_h)
     targets = (pair_in, forcing, start, mu_cols, mu_rows, table, pair_out)
     loads = [pltpu.make_async_copy(a, b, load_s.at[i]) for i, (a, b) in enumerate(zip(sources, targets))]
-    for load in loads:
+    for load in loads[:2]:
         load.start()
 
     barrier = pltpu.get_barrier_semaphore()
@@ -81,7 +82,7 @@
     def hello(device):
         pl.semaphore_signal(barrier, inc=1, device_id=device, device_id_type=MESH)
 
-    for k in zorder:
+    for k in (1, nz - 1):
         hello({"tm_1": lax.rem(z + k, nz)})
     for k in range(1, nx):
         hello({"tm_0": lax.rem(x + k, nx)})
@@ -96,6 +97,20 @@
     @pl.when(core == 0)
     def _():
         hello(place(before))
+
+    for load in loads[2:]:
+        load.start()
+    rounds = (nz // 2).bit_length() - 1
+
+    def tell(r):
+        if r < rounds:
+            for k in (2**r, nz - 2**r):
+                to = {"tm_1": lax.rem(z + k, nz)}
+                pl.semaphore_signal(known_s.at[r], inc=1, device_id=to, device_id_type=MESH)
+
+    def told(r):
+        if r < rounds:
+            pl.semaphore_wait(known_s.at[r], 2)
 
     def remote(s, d, ss, rs, device):
         return pltpu.make_async_remote_copy(
@@ -131,9 +146,10 @@
     for load in loads[:2]:
         load.wait()
     column_transform(0)
-    pl.semaphore_wait(barrier, (nz - 1) + (nx - 1) + (ny - 1) + 2)
-    for k in range(1, ny):
+    pl.semaphore_wait(barrier, 2 + (nx - 1) + (ny - 1) + 2)
+    for k in yorder:
         yf(0, k).start()
+    tell(0)
 
     @pl.when(first)
     def _():
@@ -145,8 +161,10 @@
             y0(k).start()
 
     column_transform(1)
-    for k in range(1, ny):
+    for k in yorder:
         yf(1, k).start()
+    told(0)
+    tell(1)
     rbuf[0, y] = sbuf[0, y]
     rbuf[1, y] = sbuf[1, y]
 
@@ -214,50 +232,81 @@
         hz[k] = power
         cz[k] = mix
         power, mix = power * chip_gain, mix * chip_gain + power * chip_mix
-
-    u0[...] = jnp.zeros_like(u0)
-
-    @pl.when(first)
-    def _():
-        for k in range(1, ny):
-            y0_from(k).wait_recv()
-        r0buf[y] = s0buf[y]
-        u0[...] = jnp.dot(table[0], r0buf[...].reshape(n, 128), preferred_element_type=f32)
-
-    for h in range(2):
-        for k in range(1, ny):
-            yf_from(h, k).wait_recv()
-        src[h] = jnp.dot(table[0], rbuf[h].reshape(n, 512), preferred_element_type=f32)
-
-    def relax(i, carry):
-        rows = pl.ds(pl.multiple_of(i * ROWS, ROWS), ROWS)
-        g = cf[GAIN, rows, :]
-        ends = []
-        for h in range(2):
+    told(1)
+    tell(2)
+
+    def correct(m, top, entry, r):
+        p1 = m * entry + r[0]
+        p2 = m * p1 + r[1]
+        p3 = m * p2 + r[2]
+        q = m * (m * (m * r[0] + r[1]) + r[2]) + r[3]
+        return [p1, p2, p3, top * entry + q]
+
+    def iterations(rows, b, b4p, bkp, e1, e2):
+        a, m, top = cf[A4, rows, :], cf[MID, rows, :], cf[TOP, rows, :]
+        dif, gm = cf[DIF, rows, :], cf[GM, rows, :]
+        d4p = cf[KG, rows, :] * e1 + bkp
+        r1 = [a * b4p, a * b[0], a * b[1], a * b[2]]
+        k1 = correct(m, top, e1, r1)
+        v1 = [b[c] + k1[c] for c in range(4)]
+        d = [dif * e1, dif * k1[0], dif * k1[1], dif * k1[2] - gm * e1]
+        r2 = [a * d4p, a * d[0], a * d[1], a * d[2]]
+        k2 = correct(m, top, e2, r2)
+        v2 = [v1[c] + d[c] + k2[c] for c in range(4)]
+        v0 = b4p + e1 + d4p + e2
+        return r1, k1, v1, r2, k2, v2, v0
+
+    def paired(points, h):
+        at = jnp.where(low_lanes, points[2 * h], swap(points[2 * h + 1]))
+        end = jnp.where(low_lanes, points[2 * h + 1], swap(points[2 * h + 2]))
+        return at, end
+
+
+    def relax(h, start_row, parts):
+        for i in range(parts):
+            rows = pl.ds(pl.multiple_of(start_row + i * ROWS, ROWS), ROWS)
+            g = cf[GAIN, rows, :]
             v = None
             for j in range(4):
                 s = g * src[h, rows, 128 * j : 128 * j + 128]
                 src[h, rows, 128 * j : 128 * j + 128] = s
                 v = s if v is None else g * v + s
-            ends.append(v)
-        va, vb = ends
-        va = va + cf[A4, rows, :] * u0[rows, :]
-        ab[0, rows, :] = va
-        ab[1, rows, :] = vb
-        tt[rows, :] = (
-            cf[U1, rows, :] * va + cf[U2, rows, :] * swap(va) + cf[U3, rows, :] * vb + cf[U4, rows, :] * swap(vb)
-        )
-        return carry
-
-    lax.fori_loop(0, n // ROWS, relax, 0)
-
-    own = pl.ds(pl.multiple_of(core * half_n, half_n), half_n)
-    other = pl.ds(pl.multiple_of((1 - core) * half_n, half_n), half_n)
+            if h == 0:
+                v = v + cf[A4, rows, :] * u0[rows, :]
+            w = swap(v)
+            ab[h, rows, :] = v
+            ab[2 + h, rows, :] = w
+            t = cf[U1 + 2 * h, rows, :] * v + cf[U2 + 2 * h, rows, :] * w
+            tt[rows, :] = t if h == 0 else tt[rows, :] + t
+
+    own_row = pl.multiple_of(core * half_n, half_n)
+    other_row = pl.multiple_of((1 - core) * half_n, half_n)
+    own, other = pl.ds(own_row, half_n), pl.ds(other_row, half_n)
+    u0[...] = jnp.zeros_like(u0)
+
+    for k in range(1, ny):
+        yf_from(0, k).wait_recv()
+    src[0] = jnp.dot(table[0], rbuf[0].reshape(n, 512), preferred_element_type=f32)
+
+    @pl.when(first)
+    def _():
+        for k in range(1, ny):
+            y0_from(k).wait_recv()
+        r0buf[y] = s0buf[y]
+        u0[...] = jnp.dot(table[0], r0buf[...].reshape(n, 128), preferred_element_type=f32)
+
+    relax(0, 0, n // ROWS)
+    for k in range(1, ny):
+        yf_from(1, k).wait_recv()
+    src[1] = jnp.dot(table[0], rbuf[1].reshape(n, 512), preferred_element_type=f32)
+    relax(1, other_row, half_n // ROWS)
+
     join = remote(tt.at[other], cbuf, dsend_s.at[0], drecv_s.at[0], partner)
     join.start()
+    relax(1, own_row, half_n // ROWS)
 
     wide = lax.broadcasted_iota(jnp.int32, (half_n, 128), 1) < 64
-    nsend[0] = jnp.where(wide, swap(ab[1, 0:half_n, :]), ab[1, half_n:n, :])
+    nsend[0] = jnp.where(wide, ab[3, 0:half_n, :], ab[1, half_n:n, :])
 
     def pass_on(k):
         return remote(nsend.at[k], nbuf.at[k], nsend_s.at[k], nrecv_s.at[k], place(after))
@@ -286,6 +335,7 @@
         frm = lax.rem(z + nz - k, nz)
         return remote(tc.at[frm], zbuf.at[frm], zsend_s.at[k], zrecv_s.at[k], {"tm_1": frm})
 
+    told(2)
     for k in zorder:
         zs(k).start()
     zbuf[z] = tc[z]
@@ -304,10 +354,9 @@
         v = nbuf[0, rows, :]
 
         def part(r, b4p):
-            va, vb = ab[0, r, :], ab[1, r, :]
             ga2 = cf[GA2, r, :]
-            out = cf[F4, r, :] * b4p + cf[MID, r, :] * ga2 * va + ga2 * swap(va)
-            return out - cf[KG, r, :] * cf[A4, r, :] * vb
+            out = cf[F4, r, :] * b4p + cf[MID, r, :] * ga2 * ab[0, r, :] + ga2 * ab[2, r, :]
+            return out - cf[KG, r, :] * cf[A4, r, :] * ab[1, r, :]
 
         nsend[1, rows, :] = jnp.where(low_lanes, part(rows, v), swap(part(top_rows, swap(v))))
         return carry
@@ -317,6 +366,21 @@
     @pl.when(jnp.logical_not(last))
     def _():
         pass_on(1).start()
+
+    def responses(i, carry):
+        rows = pl.ds(pl.multiple_of(i * ROWS, ROWS), ROWS)
+        g = cf[GAIN, rows, :]
+        none, unit = jnp.zeros_like(g), jnp.ones_like(g)
+        for ref, e1, e2 in ((xc, unit, none), (yc, none, unit)):
+            _, _, _, _, _, v2, v0 = iterations(rows, [none] * 4, none, none, e1, e2)
+            for h in range(2):
+                at, end = paired([v0] + v2, h)
+                for j in range(4):
+                    at = g * at if j < 3 else end
+                    ref[h, rows, 128 * j : 128 * j + 128] = at
+        return carry
+
+    lax.fori_loop(0, n // ROWS, responses, 0)
 
     for k in range(1, nz):
         zs_from(k).wait_recv()
@@ -364,6 +428,32 @@
     for k in zorder:
         es(k).start()
     ebuf[z] = esend[z]
+
+    @pl.when(jnp.logical_not(first))
+    def _():
+        pass_on(1).wait_recv()
+
+    def neighbours(i, rows):
+        b4p, bkp = unpack(0, i, rows), unpack(1, i, rows)
+        b = [ab[0, rows, :], ab[2, rows, :], ab[1, rows, :], ab[3, rows, :]]
+        return b, b4p, bkp, cf[W3, rows, :] * b4p, cf[W3, rows, :] * bkp + cf[B4, rows, :] * b4p
+
+    def still(i, carry):
+        rows = pl.ds(pl.multiple_of(i * ROWS, ROWS), ROWS)
+        b, b4p, bkp, c1, c2 = neighbours(i, rows)
+        _, _, _, _, _, v2, v0 = iterations(rows, b, b4p, bkp, -c1, -c2)
+        points = [jnp.where(first, u0[rows, :], v0)] + v2
+        g = cf[GAIN, rows, :]
+        for h in range(2):
+            at, end = paired(points, h)
+            for j in range(4):
+                lanes = slice(128 * j, 128 * j + 128)
+                at = g * at + src[h, rows, lanes] if j < 3 else end
+                src[h, rows, lanes] = at
+        return carry
+
+    lax.fori_loop(0, n // ROWS, still, 0)
+
     for k in range(1, nz):
         es_from(k).wait_recv()
 
@@ -376,59 +466,18 @@
     give.wait_recv()
     est[other, :] = fbuf[...]
 
-    @pl.when(jnp.logical_not(first))
-    def _():
-        pass_on(1).wait_recv()
-
-    def entries(i, rows):
-        b4p, bkp = unpack(0, i, rows), unpack(1, i, rows)
-        v = est[rows, :]
-        e1 = v - cf[W3, rows, :] * b4p
-        e2 = swap(v) - cf[W3, rows, :] * bkp - cf[B4, rows, :] * b4p
-        return b4p, e1, e2, cf[KG, rows, :] * e1 + bkp
-
-    def iterations(i, rows):
-        a, m, top = cf[A4, rows, :], cf[MID, rows, :], cf[TOP, rows, :]
-        dif, gm = cf[DIF, rows, :], cf[GM, rows, :]
-        b4p, e1, e2, d4p = entries(i, rows)
-        va, vb = ab[0, rows, :], ab[1, rows, :]
-        b = [va, swap(va), vb, swap(vb)]
-        r1 = [a * b4p, a * b[0], a * b[1], a * b[2]]
-
-        def correct(entry, r):
-            p1 = m * entry + r[0]
-            p2 = m * p1 + r[1]
-            p3 = m * p2 + r[2]
-            q = m * (m * (m * r[0] + r[1]) + r[2]) + r[3]
-            return [p1, p2, p3, top * entry + q]
-
-        k1 = correct(e1, r1)
-        v1 = [b[c] + k1[c] for c in range(4)]
-        d = [dif * e1, dif * k1[0], dif * k1[1], dif * k1[2] - gm * e1]
-        r2 = [a * d4p, a * d[0], a * d[1], a * d[2]]
-        k2 = correct(e2, r2)
-        v2 = [v1[c] + d[c] + k2[c] for c in range(4)]
-        v0 = b4p + e1 + d4p + e2
-        return r1, k1, v1, r2, k2, v2, v0
-
-    def path(i, carry):
-        rows = pl.ds(pl.multiple_of(i * ROWS, ROWS), ROWS)
-        _, _, _, _, _, v2, v0 = iterations(i, rows)
-        v0 = jnp.where(first, u0[rows, :], v0)
-        g = cf[GAIN, rows, :]
-        points = [v0] + v2
-        for h in range(2):
-            at = jnp.where(low_lanes, points[2 * h], swap(points[2 * h + 1]))
-            end = jnp.where(low_lanes, points[2 * h + 1], swap(points[2 * h + 2]))
+    def path(h):
+        for i in range(n // ROWS):
+            rows = slice(i * ROWS, i * ROWS + ROWS)
+            v = est[rows, :]
+            w = swap(v)
+            sx, sy = jnp.where(low_lanes, v, w), jnp.where(low_lanes, w, v)
             for j in range(4):
                 lanes = slice(128 * j, 128 * j + 128)
-                at = g * at + src[h, rows, lanes] if j < 3 else end
+                at = src[h, rows, lanes] + xc[h, rows, lanes] * sx + yc[h, rows, lanes] * sy
                 high = at.astype(bf16)
                 phi[h, rows, lanes] = high
                 plo[h, rows, lanes] = (at - high.astype(f32)).astype(bf16)
-        return carry
-
-    lax.fori_loop(0, n // ROWS, path, 0)
 
     def og(h, k):
         to = lax.rem(y + k, ny)
@@ -439,11 +488,12 @@
         return remote(obuf.at[h, frm], gbuf.at[h, frm], osend_s.at[h, k], orecv_s.at[h, k], ypeer(k))
 
     for h in range(2):
+        path(h)
         out = jnp.dot(table[0], phi[h], preferred_element_type=f32)
         out = out + jnp.dot(table[0], plo[h], preferred_element_type=f32)
         out = out + jnp.dot(table[1], phi[h], preferred_element_type=f32)
         obuf[h] = out.astype(bf16).reshape(ny, slab, 512)
-        for k in range(1, ny):
+        for k in yorder:
             og(h, k).start()
     gbuf[0, y] = obuf[0, y]
     gbuf[1, y] = obuf[1, y]
@@ -452,7 +502,9 @@
 
     def norms(i, carry):
         rows = pl.ds(pl.multiple_of(i * ROWS, ROWS), ROWS)
-        r1, k1, v1, r2, k2, v2, _ = iterations(i, rows)
+        b, b4p, bkp, c1, c2 = neighbours(i, rows)
+        v = est[rows, :]
+        r1, k1, v1, r2, k2, v2, _ = iterations(rows, b, b4p, bkp, v - c1, swap(v) - c2)
         for group, fields in enumerate((r1, r2, k1, k2, v1, v2)):
             for c in range(4):
                 at = 4 * group + c
@@ -555,9 +607,11 @@
         ((ny, slab, 128), bf16),
         ((ny, slab, 128), bf16),
         ((2, n, 512), f32),
+        ((2, n, 512), f32),
+        ((2, n, 512), f32),
         ((n, 128), f32),
         ((16, n, 128), f32),
-        ((2, n, 128), f32),
+        ((4, n, 128), f32),
         ((n, 128), f32),
         ((half_n, 128), f32),
         ((nz, zr, 128), f32),
@@ -592,7 +646,9 @@
         out_shape=tuple(pltpu.VMEM(s, f32) for s in shapes),
         in_specs=[hbm] * 7,
         out_specs=(vmem, vmem, vmem),
-        scratch_shapes=[pltpu.VMEM(s, d) for s, d in scratch] + [dma(s) for s in sems],
+        scratch_shapes=[pltpu.VMEM(s, d) for s, d in scratch]
+        + [dma(s) for s in sems]
+        + [pltpu.SemaphoreType.REGULAR((4,))],
         compiler_params=pltpu.CompilerParams(
             collective_id=0, has_side_effects=True, vmem_limit_bytes=VMEM_GRANT
         ),

time: 59.2 us -> 53.2 us (0.90)
  Pallas kernels: 58.4 us -> 52.4 us
    pallas_call x1, Pallas kernels: 57.4 us -> 51.4 us  [per_device(): pl.pallas_call(functools.partial(kernel, dims), out_shape=tuple((pltpu.VM...]
where the time goes in v3:
time: 53.2 us; the launch traced here: 53 us
  Pallas kernels  52.4 us (98%)
  between operations  0.64 us (1%)
    pallas_call x1, Pallas kernels, per_device(): pl.pallas_call(functools.partial(kernel, dims), out_shape=tuple((pltpu.VM...  51.4 us

profile of v3, /device:TPU:1, one launch (start us, length us, event | category | flops | bytes accessed | tf_op | source)
XLA Modules:
  0.0 53.0 jit_solution(8300116667648497960)
XLA Ops:
  0.6 51.4 %shard_map.94 = (f32[16,64,256]{2,1,0:T(8,128)S(1)}, f32[2,4]{1,0:T(2,128)S(1)}, f32[2,4]{1,0:T(2,128)S(1)}) custom-call(bf16[16,64,256]{2,1,0:T(8,128)(2,1)} %forcing_h.1, bf16[64,256]{1,0:T(8,128)(2,1)} %start_h.1, bf16[2,256,512]{2,1,0:T(8,128)(2,1)} %constant.10.clone.pair_in_h, bf16[2,512,256]{2,1,0:T(8,128)(2,1)} %constant.11.clone.pair_out_h, ...), custom_call_target="tpu_custom_call" | custom-call | tf_op jit(solution)/shard_map/pallas_call | solution.py:644
  52.0 1.0 %shard_map.95 = (f32[16,64,256]{2,1,0:T(8,128)}, f32[2,4]{1,0:T(2,128)}, f32[2,4]{1,0:T(2,128)}) custom-call(f32[16,64,256]{2,1,0:T(8,128)S(1)} %get-tuple-element.6.heat_v, f32[2,4]{1,0:T(2,128)S(1)} %get-tuple-element.7.history_v, f32[2,4]{1,0:T(2,128)S(1)} %get-tuple-element.8.change_v), custom_call_target="tpu_custom_call" | custom-call | tf_op jit(solution)/shard_map/pallas_call | solution.py:656

commit v4 on v3

--- a/solution.py
+++ b/solution.py
@@ -17,7 +17,6 @@
 TM = ("tm_0", "tm_1", "tm_2")
 
 GAIN, A4, MID, TOP, DIF, KG, GM, W3, C0, F4, GA2, U1, U2, U3, U4, B4 = range(16)
-
 
 def tables(n, ny):
     w = n // ny
@@ -36,10 +35,8 @@
     back = np.ascontiguousarray(np.swapaxes(pair, 1, 2))
     return pair, back, np.stack([half, low]), mu_rows, mu_cols
 
-
 def swap(v):
     return pltpu.roll(v, 64, 1)
-
 
 def kernel(
     dims,
@@ -261,7 +258,6 @@
         end = jnp.where(low_lanes, points[2 * h + 1], swap(points[2 * h + 2]))
         return at, end
 
-
     def relax(h, start_row, parts):
         for i in range(parts):
             rows = pl.ds(pl.multiple_of(start_row + i * ROWS, ROWS), ROWS)
@@ -466,39 +462,20 @@
     give.wait_recv()
     est[other, :] = fbuf[...]
 
-    def path(h):
+    def path(q):
+        h, first_step = q // 2, 2 * (q % 2)
         for i in range(n // ROWS):
             rows = slice(i * ROWS, i * ROWS + ROWS)
             v = est[rows, :]
             w = swap(v)
             sx, sy = jnp.where(low_lanes, v, w), jnp.where(low_lanes, w, v)
-            for j in range(4):
+            for j in range(first_step, first_step + 2):
                 lanes = slice(128 * j, 128 * j + 128)
                 at = src[h, rows, lanes] + xc[h, rows, lanes] * sx + yc[h, rows, lanes] * sy
                 high = at.astype(bf16)
                 phi[h, rows, lanes] = high
                 plo[h, rows, lanes] = (at - high.astype(f32)).astype(bf16)
 
-    def og(h, k):
-        to = lax.rem(y + k, ny)
-        return remote(obuf.at[h, to], gbuf.at[h, y], osend_s.at[h, k], orecv_s.at[h, k], ypeer(k))
-
-    def og_from(h, k):
-        frm = lax.rem(y + ny - k, ny)
-        return remote(obuf.at[h, frm], gbuf.at[h, frm], osend_s.at[h, k], orecv_s.at[h, k], ypeer(k))
-
-    for h in range(2):
-        path(h)
-        out = jnp.dot(table[0], phi[h], preferred_element_type=f32)
-        out = out + jnp.dot(table[0], plo[h], preferred_element_type=f32)
-        out = out + jnp.dot(table[1], phi[h], preferred_element_type=f32)
-        obuf[h] = out.astype(bf16).reshape(ny, slab, 512)
-        for k in yorder:
-            og(h, k).start()
-    gbuf[0, y] = obuf[0, y]
-    gbuf[1, y] = obuf[1, y]
-
-    stat[...] = jnp.zeros_like(stat)
 
     def norms(i, carry):
         rows = pl.ds(pl.multiple_of(i * ROWS, ROWS), ROWS)
@@ -512,8 +489,6 @@
                 stat[at : at + 1, :] = stat[at : at + 1, :] + jnp.sum(sq, axis=0, keepdims=True)
         return carry
 
-    lax.fori_loop(0, n // ROWS, norms, 0)
-
     def ts(k):
         return remote(stat, stbuf.at[y], tsend_s.at[k], trecv_s.at[k], ypeer(k))
 
@@ -521,24 +496,46 @@
         frm = lax.rem(y + ny - k, ny)
         return remote(stat, stbuf.at[frm], tsend_s.at[k], trecv_s.at[k], ypeer(k))
 
-    for k in range(1, ny):
-        ts(k).start()
+    def og(h, k):
+        to = lax.rem(y + k, ny)
+        return remote(obuf.at[h, to], gbuf.at[h, y], osend_s.at[h, k], orecv_s.at[h, k], ypeer(k))
+
+    def og_from(h, k):
+        frm = lax.rem(y + ny - k, ny)
+        return remote(obuf.at[h, frm], gbuf.at[h, frm], osend_s.at[h, k], orecv_s.at[h, k], ypeer(k))
+
+    for q in range(4):
+        path(q)
+        h, lanes = q // 2, slice(256 * (q % 2), 256 * (q % 2) + 256)
+        out = jnp.dot(table[0], phi[h, :, lanes], preferred_element_type=f32)
+        out = out + jnp.dot(table[0], plo[h, :, lanes], preferred_element_type=f32)
+        out = out + jnp.dot(table[1], phi[h, :, lanes], preferred_element_type=f32)
+        obuf[q] = out.astype(bf16).reshape(ny, slab, 256)
+        for k in yorder:
+            og(q, k).start()
+        if q == 1:
+            stat[...] = jnp.zeros_like(stat)
+            lax.fori_loop(0, n // ROWS, norms, 0)
+            for k in yorder:
+                ts(k).start()
+    for q in range(4):
+        gbuf[q, y] = obuf[q, y]
     stbuf[y] = stat[...]
 
-    for h in range(2):
+    for q in range(4):
         for k in range(1, ny):
-            og_from(h, k).wait_recv()
+            og_from(q, k).wait_recv()
+        lhs = jnp.concatenate(
+            [
+                jnp.concatenate([gbuf[q, s, :, 128 * j : 128 * j + 128] for s in range(ny)], axis=1)
+                for j in range(2)
+            ],
+            axis=0,
+        )
         for p in range(2):
-            lhs = jnp.concatenate(
-                [
-                    jnp.concatenate([gbuf[h, s, :, 128 * j : 128 * j + 128] for s in range(ny)], axis=1)
-                    for j in range(4)
-                ],
-                axis=0,
-            )
             out = jnp.dot(lhs, pair_out[p], preferred_element_type=f32)
-            for j in range(4):
-                heat[8 * h + 4 * p + j] = out[j * slab : (j + 1) * slab, :]
+            for j in range(2):
+                heat[8 * (q // 2) + 4 * p + 2 * (q % 2) + j] = out[j * slab : (j + 1) * slab, :]
 
     for k in range(1, ny):
         ts_from(k).wait_recv()
@@ -558,7 +555,8 @@
     for k in range(1, ny):
         for h in range(2):
             yf(h, k).wait_send()
-            og(h, k).wait_send()
+        for q in range(4):
+            og(q, k).wait_send()
         ts(k).wait_send()
 
     @pl.when(first)
@@ -580,15 +578,14 @@
     for k in range(1, nx):
         xs(k).wait_send()
 
-
 def store(heat_v, history_v, change_v, heat, history, change, sems):
-    pairs = ((heat_v, heat), (history_v, history), (change_v, change))
+    cut = [pl.ds(4 * i, 4) for i in range(STEPS // 4)]
+    pairs = [(heat_v.at[c], heat.at[c]) for c in cut] + [(history_v, history), (change_v, change)]
     copies = [pltpu.make_async_copy(a, b, sems.at[i]) for i, (a, b) in enumerate(pairs)]
     for copy in copies:
         copy.start()
     for copy in copies:
         copy.wait()
-
 
 def per_device(dims, forcing, starting_heat):
     nx, nz, nc, ny, n = dims
@@ -629,14 +626,14 @@
         ((n, 128), f32),
         ((2, n, 512), bf16),
         ((2, n, 512), bf16),
-        ((2, ny, slab, 512), bf16),
-        ((2, ny, slab, 512), bf16),
+        ((4, ny, slab, 256), bf16),
+        ((4, ny, slab, 256), bf16),
         ((24, 128), f32),
         ((ny, 24, 128), f32),
     ]
     sems = [
         (2, ny), (2, ny), (ny,), (ny,), (2,), (2,), (2,), (2,), (nz,), (nz,),
-        (nx,), (nx,), (nz,), (nz,), (2, ny), (2, ny), (ny,), (ny,), (7,),
+        (nx,), (nx,), (nz,), (nz,), (4, ny), (4, ny), (ny,), (ny,), (7,),
     ]
     vmem = pl.BlockSpec(memory_space=pltpu.VMEM)
     hbm = pl.BlockSpec(memory_space=pltpu.HBM)
@@ -658,10 +655,9 @@
         out_shape=tuple(jax.ShapeDtypeStruct(s, f32) for s in shapes),
         in_specs=[vmem] * 3,
         out_specs=(hbm, hbm, hbm),
-        scratch_shapes=[dma((3,))],
+        scratch_shapes=[dma((STEPS // 4 + 2,))],
         compiler_params=pltpu.CompilerParams(vmem_limit_bytes=4 * 1024 * 1024),
     )(*held)
-
 
 def build(mesh, nx, nz, nc, n):
     ny = mesh.shape["space"]
@@ -674,6 +670,5 @@
         check_vma=False,
     )
 
-
 def solution(mesh):
     return build(mesh, 4, 16, 2, 256)

time: 53.2 us -> 53.3 us (level)
  no operation moved by 1% of the time
where the time goes in v4:
time: 53.3 us; the launch traced here: 53.1 us
  Pallas kernels  52.5 us (98%)
  between operations  0.64 us (1%)
    pallas_call x1, Pallas kernels, per_device(): pl.pallas_call(functools.partial(kernel, dims), out_shape=tuple((pltpu.VM...  51.5 us

profile of v4, /device:TPU:1, one launch (start us, length us, event | category | flops | bytes accessed | tf_op | source)
XLA Modules:
  0.0 53.1 jit_solution(7636968447187507719)
XLA Ops:
  0.6 51.5 %shard_map.94 = (f32[16,64,256]{2,1,0:T(8,128)S(1)}, f32[2,4]{1,0:T(2,128)S(1)}, f32[2,4]{1,0:T(2,128)S(1)}) custom-call(bf16[16,64,256]{2,1,0:T(8,128)(2,1)} %forcing_h.1, bf16[64,256]{1,0:T(8,128)(2,1)} %start_h.1, bf16[2,256,512]{2,1,0:T(8,128)(2,1)} %constant.10.clone.pair_in_h, bf16[2,512,256]{2,1,0:T(8,128)(2,1)} %constant.11.clone.pair_out_h, ...), custom_call_target="tpu_custom_call" | custom-call | tf_op jit(solution)/shard_map/pallas_call | solution.py:641
  52.1 1.0 %shard_map.95 = (f32[16,64,256]{2,1,0:T(8,128)}, f32[2,4]{1,0:T(2,128)}, f32[2,4]{1,0:T(2,128)}) custom-call(f32[16,64,256]{2,1,0:T(8,128)S(1)} %get-tuple-element.6.heat_v, f32[2,4]{1,0:T(2,128)S(1)} %get-tuple-element.7.history_v, f32[2,4]{1,0:T(2,128)S(1)} %get-tuple-element.8.change_v), custom_call_target="tpu_custom_call" | custom-call | tf_op jit(solution)/shard_map/pallas_call | solution.py:653
